TPU v7x, 256 devices: a whole 4x4x8 slice. The times are simulated.
256 devices in a mesh: frow: 16 (over x_lo, y, core), fcol: 16 (over z, x_hi).
Axes of the slice: x: 4 (x_hi: 2, x_lo: 2; x = x_hi * 2 + x_lo), y: 4, z: 8, core: 2. Of those that a mesh axis runs over, the one named last changes fastest.
Arguments:
- facets: float32 [2, 16384, 16384], P(None, 'frow', 'fcol'), may hold values from -6 to 6
- facet_row_offset: int32 [16], P('frow'), may hold values from 0 to 16383
- facet_col_offset: int32 [16], P('fcol'), may hold values from 0 to 16383
- strip_offset: int32 [4], replicated, may hold values from 0 to 16383
- subgrid_strip: int32 [48], replicated, may hold values from 0 to 3
- subgrid_column: int32 [48], replicated, may hold values from 0 to 16383
- subgrid_slot: int32 [48], replicated, may hold values from 0 to 47, each once
Outputs:
- subgrids: float32 [48, 2, 128, 128], P('frow', None, 'fcol')
Inputs may be any that keep to these rules, and one draw needn't show every extreme that they name: `subgrid_slot`: every slot from 0 to 47 is named by exactly one subgrid.
All inputs are finite; a program needn't handle non-finite values.
Results may differ from a plain program's by a relative error of at most 0.0003.
Values sent between devices are 32-bit elements; how exact they have to be, the bound alone decides.
A program may use at most 64 MiB of HBM per device.

v0:
```python
import math

import jax
import jax.numpy as jnp
from jax import lax
from jax.experimental import pallas as pl
from jax.experimental.pallas import tpu as pltpu
from jax.sharding import PartitionSpec as P

F = 1024
M = 128
N = 16384
MASK = N - 1
SLOTS = 48
CW = 256
NT = F // CW
f32 = jnp.float32
bf16 = jnp.bfloat16
MESH = pl.DeviceIdType.MESH

FLIP = (8, 2, 6)
ORDERS = ((0, 1, 2), (1, 2, 0), (2, 0, 1))


def groups_of(u):
    cuts = ((0, 2), (2, 1), (3, 1))
    return [(ORDERS[(u + g) % 3], c0, n) for g, (c0, n) in enumerate(cuts)]


def iota(shape, dim):
    return lax.broadcasted_iota(jnp.int32, shape, dim)


def cos_sin(m):
    q = (m + N // 8) >> 12
    x = (m - (q << 12)).astype(f32) * (2.0 * math.pi / N)
    x2 = x * x
    s = x * (1.0 + x2 * (-1.0 / 6 + x2 * (1.0 / 120 + x2 * (-1.0 / 5040 + x2 * (1.0 / 362880)))))
    c = 1.0 + x2 * (-0.5 + x2 * (1.0 / 24 + x2 * (-1.0 / 720 + x2 * (1.0 / 40320))))
    swap = (q & 1) == 1
    cos = jnp.where(swap, s, c)
    sin = jnp.where(swap, c, s)
    cos = jnp.where(((q + 1) & 2) == 2, -cos, cos)
    sin = jnp.where((q & 2) == 2, -sin, sin)
    return cos, sin


def window(j):
    x = (jnp.minimum(j, F - 1 - j).astype(f32) + 0.5) * (math.pi / F)
    x2 = x * x
    poly = 1.0 / 6227020800
    for k in (-39916800, 362880, -5040, 120, -6, 1):
        poly = poly * x2 + 1.0 / k
    return poly * x * (1.0 / math.sqrt(N))


def split(x):
    hi = x.astype(bf16)
    return hi, (x - hi.astype(f32)).astype(bf16)


def dot3(ah, al, bh, bl):
    def d(a, b):
        return jnp.dot(a, b, preferred_element_type=f32)

    return d(ah, bh) + d(ah, bl) + d(al, bh)


def kernel(
    x_hbm, roff, coff, soff, strip_of, col_of, out_ref,
    xf, xh, xl, th, tl, ut, vt, s, rd, r0, r1, r2,
    fb, ph, eh, el, ah, al, gacc, g, ra, pb, rb,
    x_sem, d_ssem, d_rsem, e_ssem, e_rsem, a_ssem, a_rsem, b_ssem, b_rsem,
):
    i = lax.axis_index("frow")
    j = lax.axis_index("fcol")
    core = i & 1
    y = (i >> 1) & 3
    xlo = i >> 3
    z = j >> 1
    xhi = j & 1
    own = (xlo, (y ^ (y >> 1)) & 1, y >> 1)
    kz = own[0] * 4 + own[1] * 2 + own[2]
    recv_bufs = (r0, r1, r2)

    def x_copy(t):
        return pltpu.make_async_copy(
            x_hbm.at[:, :, pl.ds(t * CW, CW)], xf.at[t], x_sem.at[t]
        )

    for t in range(NT):
        x_copy(t).start()

    barrier = pltpu.get_barrier_semaphore()

    def hello(fr, fc):
        pl.semaphore_signal(barrier, inc=1, device_id=(fr, fc), device_id_type=MESH)

    for flip in (1, *FLIP):
        hello(i ^ flip, j)

    @pl.loop(0, 8)
    def _(p):
        for xs in range(2):
            src_i = p * 2 + xhi
            src_j = z * 2 + xs

            @pl.when(jnp.logical_or(src_i != i, src_j != j))
            def _():
                hello(src_i, src_j)

        @pl.when(p != z)
        def _():
            hello(i, p * 2 + xhi)

    def wait_barrier():
        pl.semaphore_wait(barrier, 27 - (1 - (core ^ xhi)))

    def gen_u():
        row = iota((64, 1), 0)
        c = row & 3
        kb = row >> 2
        block = ((kb & 7) << 1) | (kb >> 3)
        f = jnp.where(c == 0, soff[0], jnp.where(c == 1, soff[1], jnp.where(c == 2, soff[2], soff[3])))
        f = f + 8 * block
        for b in range(4):
            p = roff[0] + b * 256 + iota((1, 256), 1)
            cos, sin = cos_sin((f * p) & MASK)
            ut[0, :, b * 256 : (b + 1) * 256] = cos
            ut[1, :, b * 256 : (b + 1) * 256] = sin

    def gen_t(h):
        r = iota((8, 1), 0)
        jj = iota((1, F), 1)
        m = ((r & 3) + 4 * h) * (roff[0] + jj) + (r >> 2) * (N // 4)
        cos, sin = cos_sin(m & MASK)
        w = window(jj)
        vt[0] = w * cos
        vt[1] = w * sin

        for b in range(4):
            cols = slice(b * 256, (b + 1) * 256)
            right = slice(F + b * 256, F + (b + 1) * 256)
            vr = vt[0, :, cols]
            vi = vt[1, :, cols]
            for kb in range(16):
                left_t, right_t = [], []
                for c in range(4):
                    q = kb * 4 + c
                    ur = ut[0, q : q + 1, cols]
                    ui = ut[1, q : q + 1, cols]
                    left_t.append(ur * vr - ui * vi)
                    right_t.append(ui * vr + ur * vi)
                hi, lo = split(jnp.concatenate(left_t, 0))
                th[h, kb, :, cols] = hi
                tl[h, kb, :, cols] = lo
                hi, lo = split(jnp.concatenate(right_t, 0))
                th[h, kb, :, right] = hi
                tl[h, kb, :, right] = lo

    def split_x(t):
        @pl.loop(0, 8)
        def _(b):
            rows = pl.ds(pl.multiple_of(b * 128, 128), 128)
            for part in range(2):
                hi, lo = split(xf[t, part, rows, :])
                dst = pl.ds(pl.multiple_of(part * F + b * 128, 128), 128)
                xh[t, dst, :] = hi
                xl[t, dst, :] = lo

    def gen_cols():
        for b in range(4):
            jj = b * 256 + iota((1, 256), 1)
            cos, sin = cos_sin((col_of[...] * (coff[0] + jj)) & MASK)
            w = window(jj)
            ph[0, :, b * 256 : (b + 1) * 256] = w * cos
            ph[1, :, b * 256 : (b + 1) * 256] = -(w * sin)

        @pl.loop(0, 32)
        def _(b):
            n = b * 32 + iota((32, 1), 0)
            m = (iota((1, M), 1) * (coff[0] + n)) & MASK
            cos, sin = cos_sin(m)
            hi, lo = split(jnp.concatenate([cos, -sin], 1))
            rows = pl.ds(pl.multiple_of(b * 32, 32), 32)
            eh[rows, :] = hi
            el[rows, :] = lo

    def matmul(u):
        h, t = divmod(u, NT)
        out = dot3(
            th[h].reshape(512, 2 * F), tl[h].reshape(512, 2 * F), xh[t], xl[t]
        )
        s[u] = out.reshape(2, 2, 2, 2, 4, 8, CW)

    def d2d(u):
        return pltpu.make_async_remote_copy(
            src_ref=s.at[u, 1 - core],
            dst_ref=rd.at[u],
            send_sem=d_ssem.at[u],
            recv_sem=d_rsem.at[u],
            device_id=(i ^ 1, j),
            device_id_type=MESH,
        )

    def region(order, k, c0, n, other):
        sel = [slice(None)] * 3
        for d in order[:k]:
            sel[d] = own[d]
        sel[order[k]] = 1 - own[order[k]] if other else own[order[k]]
        return (*sel, slice(c0, c0 + n))

    def exchange(u, k, gi):
        order, c0, n = groups_of(u)[gi]
        return pltpu.make_async_remote_copy(
            src_ref=s.at[(u, core, *region(order, k, c0, n, True))],
            dst_ref=recv_bufs[k].at[(u, *[slice(None)] * (2 - k), slice(c0, c0 + n))],
            send_sem=e_ssem.at[u, k, gi],
            recv_sem=e_rsem.at[u, k, gi],
            device_id=(i ^ FLIP[order[k]], j),
            device_id_type=MESH,
        )

    def finish_d2d(u):
        d2d(u).wait_recv()
        s[u, core] += rd[u]
        for gi in range(3):
            exchange(u, 0, gi).start()

    def finish_exchange(u, k):
        for gi, (order, c0, n) in enumerate(groups_of(u)):
            exchange(u, k, gi).wait_recv()
            at = (u, core, *region(order, k, c0, n, False))
            s[at] += recv_bufs[k][(u, *[slice(None)] * (2 - k), slice(c0, c0 + n))]
            if k < 2:
                exchange(u, k + 1, gi).start()

    sign = jnp.where(iota((8, 1), 0) < 4, -1.0, 1.0).astype(f32)

    def columns(u):
        h, t = divmod(u, NT)
        cols = slice(t * CW, (t + 1) * CW)
        for c in range(4):
            tile = s[u, core, own[0], own[1], own[2], c]
            fb[0, c] = tile
            fb[1, c] = jnp.concatenate([tile[4:], tile[:4]], 0) * sign
        for q0 in range(0, SLOTS, 4):
            tiles = []
            for q in range(q0, q0 + 4):
                st = strip_of[q]
                tiles.append(fb[0, st] * ph[0, q : q + 1, cols] + fb[1, st] * ph[1, q : q + 1, cols])
            hi, lo = split(jnp.concatenate(tiles, 0))
            ah[q0 * 8 : (q0 + 4) * 8, :] = hi
            al[q0 * 8 : (q0 + 4) * 8, :] = lo
        prod = dot3(ah[...], al[...], eh[cols, :], el[cols, :])
        if t == 0:
            gacc[...] = prod
        elif t < NT - 1:
            gacc[...] += prod
        else:
            total = (gacc[...] + prod).reshape(SLOTS, 8, 2 * M)
            cross = total[:, :, M:]
            cross = jnp.concatenate([cross[:, 4:], cross[:, :4]], 1)
            g[h] = total[:, :, :M] + cross * sign

    def a_copy(h, a):
        return pltpu.make_async_remote_copy(
            src_ref=g.at[h, pl.ds(3 * a, 3)],
            dst_ref=ra.at[h, xhi, kz],
            send_sem=a_ssem.at[h, a],
            recv_sem=a_rsem.at[h, xhi, kz],
            device_id=(a, z * 2 + core),
            device_id_type=MESH,
        )

    def a_remote(a):
        return jnp.logical_or(a != i, core != xhi)

    def start_a(h):
        @pl.loop(0, 16)
        def _(n):
            a = (n + i) & 15

            @pl.when(a_remote(a))
            def _():
                a_copy(h, a).start()

        @pl.when(core == xhi)
        def _():
            ra[h, xhi, kz] = g[h, pl.ds(3 * i, 3)]

    def b_copy(h, k):
        return pltpu.make_async_remote_copy(
            src_ref=pb.at[h, k],
            dst_ref=rb.at[h, z],
            send_sem=b_ssem.at[h, k],
            recv_sem=b_rsem.at[h, z],
            device_id=(i, k * 2 + xhi),
            device_id_type=MESH,
        )

    def a_arrival(h, xs, k):
        return pltpu.make_async_remote_copy(
            src_ref=g.at[h, pl.ds(0, 3)],
            dst_ref=ra.at[h, xs, k],
            send_sem=a_ssem.at[h, 0],
            recv_sem=a_rsem.at[h, xs, k],
            device_id=(i, j),
            device_id_type=MESH,
        )

    def b_arrival(h, zs):
        return pltpu.make_async_remote_copy(
            src_ref=pb.at[h, 0],
            dst_ref=rb.at[h, zs],
            send_sem=b_ssem.at[h, 0],
            recv_sem=b_rsem.at[h, zs],
            device_id=(i, j),
            device_id_type=MESH,
        )

    def finish_a(h):
        @pl.loop(0, 8)
        def _(n):
            k = (n + z + 1) & 7
            for xs in range(2):
                mine = jnp.logical_and(core == xhi, jnp.logical_and(xhi == xs, k == kz))

                @pl.when(jnp.logical_not(mine))
                def _():
                    a_arrival(h, xs, k).wait_recv()

            pb[h, k] = ra[h, 0, k] + ra[h, 1, k]

            @pl.when(k != z)
            def _():
                b_copy(h, k).start()

    def finish_b(h):
        rb[h, z] = pb[h, z]

        @pl.loop(0, 8)
        def _(zs):
            @pl.when(zs != z)
            def _():
                b_arrival(h, zs).wait_recv()

        total = rb[h, 0]
        for zs in range(1, 8):
            total = total + rb[h, zs]
        out_ref[:, 0, 4 * h : 4 * h + 4, :] = total[:, :4]
        out_ref[:, 1, 4 * h : 4 * h + 4, :] = total[:, 4:]

    gen_u()
    gen_t(0)
    slots = 2 * NT
    for v in range(slots + 4):
        if v < NT:
            x_copy(v).wait()
            split_x(v)
        if v == 1:
            gen_cols()
        if v == NT:
            gen_t(1)
        if v < slots:
            matmul(v)
            if v == 0:
                wait_barrier()
            d2d(v).start()
        if 0 <= v - 1 < slots:
            finish_d2d(v - 1)
        for k in range(3):
            if 0 <= v - 2 - k < slots:
                finish_exchange(v - 2 - k, k)
        if 0 <= v - 4 < slots:
            columns(v - 4)
            if v - 4 == NT - 1:
                start_a(0)
        if v == slots + 1:
            finish_a(0)
    start_a(1)
    finish_b(0)
    finish_a(1)
    finish_b(1)

    for u in range(slots):
        d2d(u).wait_send()
        for k in range(3):
            for gi in range(3):
                exchange(u, k, gi).wait_send()

    @pl.loop(0, 16)
    def _(a):
        for h in range(2):

            @pl.when(a_remote(a))
            def _():
                a_copy(h, a).wait_send()

    @pl.loop(0, 8)
    def _(k):
        for h in range(2):

            @pl.when(k != z)
            def _():
                b_copy(h, k).wait_send()


def per_device(facets, row_off, col_off, strip_offset, subgrid_strip, subgrid_column, subgrid_slot):
    ids = jnp.arange(SLOTS, dtype=jnp.int32)
    hit = subgrid_slot[None, :] == ids[:, None]
    strip_of = jnp.sum(jnp.where(hit, subgrid_strip[None, :], 0), axis=1)
    col_of = jnp.sum(jnp.where(hit, subgrid_column[None, :], 0), axis=1, keepdims=True)
    smem = pl.BlockSpec(memory_space=pltpu.SMEM)
    vmem = pl.BlockSpec(memory_space=pltpu.VMEM)
    dma = pltpu.SemaphoreType.DMA
    u = 2 * NT
    return pl.pallas_call(
        kernel,
        out_shape=jax.ShapeDtypeStruct((3, 2, 8, M), f32),
        in_specs=[pl.BlockSpec(memory_space=pl.ANY), smem, smem, smem, smem, vmem],
        out_specs=vmem,
        scratch_shapes=[
            pltpu.VMEM((NT, 2, F, CW), f32),
            pltpu.VMEM((NT, 2 * F, CW), bf16),
            pltpu.VMEM((NT, 2 * F, CW), bf16),
            pltpu.VMEM((2, 16, 32, 2 * F), bf16),
            pltpu.VMEM((2, 16, 32, 2 * F), bf16),
            pltpu.VMEM((2, 64, F), f32),
            pltpu.VMEM((2, 8, F), f32),
            pltpu.VMEM((u, 2, 2, 2, 2, 4, 8, CW), f32),
            pltpu.VMEM((u, 2, 2, 2, 4, 8, CW), f32),
            pltpu.VMEM((u, 2, 2, 4, 8, CW), f32),
            pltpu.VMEM((u, 2, 4, 8, CW), f32),
            pltpu.VMEM((u, 4, 8, CW), f32),
            pltpu.VMEM((2, 4, 8, CW), f32),
            pltpu.VMEM((2, SLOTS, F), f32),
            pltpu.VMEM((F, 2 * M), bf16),
            pltpu.VMEM((F, 2 * M), bf16),
            pltpu.VMEM((SLOTS * 8, CW), bf16),
            pltpu.VMEM((SLOTS * 8, CW), bf16),
            pltpu.VMEM((SLOTS * 8, 2 * M), f32),
            pltpu.VMEM((2, SLOTS, 8, M), f32),
            pltpu.VMEM((2, 2, 8, 3, 8, M), f32),
            pltpu.VMEM((2, 8, 3, 8, M), f32),
            pltpu.VMEM((2, 8, 3, 8, M), f32),
            dma((NT,)),
            dma((u,)),
            dma((u,)),
            dma((u, 3, 3)),
            dma((u, 3, 3)),
            dma((2, 16)),
            dma((2, 2, 8)),
            dma((2, 8)),
            dma((2, 8)),
        ],
        compiler_params=pltpu.CompilerParams(
            collective_id=0, has_side_effects=True, vmem_limit_bytes=60 * 1024 * 1024
        ),
        name="facet_to_subgrid",
    )(facets, row_off, col_off, strip_offset, strip_of, col_of)


def solution(mesh):
    placed = (P(None, "frow", "fcol"), P("frow"), P("fcol"), P(), P(), P(), P())
    return jax.shard_map(
        per_device,
        mesh=mesh,
        in_specs=placed,
        out_specs=P("frow", None, "fcol", None),
        check_vma=False,
    )
```

profile of v0, /device:TPU:1, one launch (start us, length us, event | category | flops | bytes accessed | tf_op | source)
XLA Modules:
  0.0 74.3 jit_solution(6411611841828940407)
XLA Ops:
  1.3 1.3 %select_reduce_fusion = (s32[48]{0:T(128)S(1)}, s32[48]{0:T(128)}) fusion(s32[48]{0:T(128)} %param.12, s32[48]{0:T(128)} %param.13, s32[48]{0:T(128)} %param.11), kind=kLoop, calls=%fused_computation | loop fusion | flops 11424 | bytes 960 | tf_op jit(solution)/shard_map/reduce_sum | solution.py:413
  2.6 0.7 copy.9.col_of
  3.3 69.6 %facet_to_subgrid.1 = f32[3,2,8,128]{3,2,1,0:T(8,128)} custom-call(f32[2,1024,1024]{2,1,0:T(8,128)} %x_hbm.1, s32[1]{0:T(128)S(6)} %copy.11.roff, s32[1]{0:T(128)S(6)} %copy.12.coff, s32[4]{0:T(128)} %soff.1, s32[48]{0:T(128)} %get-tuple-element.6.strip_of, s32[48,1]{1,0:T(8,128)} %copy.9.col_of), custom_call_target="tpu_custom_call" | custom-call | tf_op jit(solution)/shard_map/facet_to_subgrid/pallas_call | solution.py:418
  72.9 1.3 %copy.13 = f32[3,2,8,128]{3,2,1,0:T(8,128)} copy(f32[3,2,8,128]{3,2,1,0:T(8,128)} %facet_to_subgrid.1) | data formatting | bytes 49152
where the time goes:
time: 74.5 us; the launch traced here: 74.3 us
  Pallas kernels  69.6 us (93%)
  local copies, waits for them, and re-layouts  2.04 us (3%)
  other arithmetic  1.34 us (2%)
  between operations  1.31 us (2%)
    pallas_call x1, Pallas kernels, per_device(): pl.pallas_call(kernel, out_shape=jax.ShapeDtypeStruct((3, 2, 8, M), f32),...  69.6 us

commit v1 on v0

--- a/solution.py
+++ b/solution.py
@@ -67,10 +67,10 @@
 
 
 def kernel(
-    x_hbm, roff, coff, soff, strip_of, col_of, out_ref,
-    xf, xh, xl, th, tl, ut, vt, s, rd, r0, r1, r2,
+    x_hbm, roff, coff, soff, g_strip, g_column, g_slot, out_ref,
+    strip_row, strip_of, col_of, xf, xh, xl, th, tl, ut, vt, s, rd, r0, r1, r2,
     fb, ph, eh, el, ah, al, gacc, g, ra, pb, rb,
-    x_sem, d_ssem, d_rsem, e_ssem, e_rsem, a_ssem, a_rsem, b_ssem, b_rsem,
+    x_sem, st_sem, d_ssem, d_rsem, e_ssem, e_rsem, a_ssem, a_rsem, b_ssem, b_rsem,
 ):
     i = lax.axis_index("frow")
     j = lax.axis_index("fcol")
@@ -99,22 +99,32 @@
     for flip in (1, *FLIP):
         hello(i ^ flip, j)
 
-    @pl.loop(0, 8)
-    def _(p):
-        for xs in range(2):
-            src_i = p * 2 + xhi
-            src_j = z * 2 + xs
-
-            @pl.when(jnp.logical_or(src_i != i, src_j != j))
-            def _():
-                hello(src_i, src_j)
-
-        @pl.when(p != z)
-        def _():
-            hello(i, p * 2 + xhi)
+    for d in range(1, 16):
+        hello((((i >> 1) ^ (d >> 1)) << 1) | xhi, z * 2 + (xhi ^ (d & 1)))
+
+    @pl.when(core != xhi)
+    def _():
+        hello(i ^ 1, j)
+
+    for d in range(1, 8):
+        hello(i, (z ^ d) * 2 + xhi)
 
     def wait_barrier():
         pl.semaphore_wait(barrier, 27 - (1 - (core ^ xhi)))
+
+    def gen_slots():
+        lane = iota((1, 128), 1)
+        row = iota((SLOTS, 1), 0)
+        strips = jnp.zeros((1, 128), jnp.int32)
+        columns_ = jnp.zeros((SLOTS, 1), jnp.int32)
+        for n in range(SLOTS):
+            strips = jnp.where(lane == g_slot[n], g_strip[n], strips)
+            columns_ = jnp.where(row == g_slot[n], g_column[n], columns_)
+        strip_row[...] = strips
+        col_of[...] = columns_
+
+    def strip_copy():
+        return pltpu.make_async_copy(strip_row, strip_of, st_sem.at[0])
 
     def gen_u():
         row = iota((64, 1), 0)
@@ -188,10 +198,12 @@
 
     def matmul(u):
         h, t = divmod(u, NT)
-        out = dot3(
-            th[h].reshape(512, 2 * F), tl[h].reshape(512, 2 * F), xh[t], xl[t]
-        )
-        s[u] = out.reshape(2, 2, 2, 2, 4, 8, CW)
+        for half in range(2):
+            rows = slice(8 * half, 8 * half + 8)
+            out = dot3(
+                th[h, rows].reshape(256, 2 * F), tl[h, rows].reshape(256, 2 * F), xh[t], xl[t]
+            )
+            s[u, half] = out.reshape(2, 2, 2, 4, 8, CW)
 
     def d2d(u):
         return pltpu.make_async_remote_copy(
@@ -247,7 +259,7 @@
         for q0 in range(0, SLOTS, 4):
             tiles = []
             for q in range(q0, q0 + 4):
-                st = strip_of[q]
+                st = strip_of[0, q]
                 tiles.append(fb[0, st] * ph[0, q : q + 1, cols] + fb[1, st] * ph[1, q : q + 1, cols])
             hi, lo = split(jnp.concatenate(tiles, 0))
             ah[q0 * 8 : (q0 + 4) * 8, :] = hi
@@ -273,21 +285,25 @@
             device_id_type=MESH,
         )
 
-    def a_remote(a):
-        return jnp.logical_or(a != i, core != xhi)
-
     def start_a(h):
-        @pl.loop(0, 16)
-        def _(n):
-            a = (n + i) & 15
-
-            @pl.when(a_remote(a))
-            def _():
-                a_copy(h, a).start()
+        for d in range(15, 0, -1):
+            a_copy(h, i ^ d).start()
+
+        @pl.when(core != xhi)
+        def _():
+            a_copy(h, i).start()
 
         @pl.when(core == xhi)
         def _():
             ra[h, xhi, kz] = g[h, pl.ds(3 * i, 3)]
+
+    def end_a(h):
+        for d in range(15, 0, -1):
+            a_copy(h, i ^ d).wait_send()
+
+        @pl.when(core != xhi)
+        def _():
+            a_copy(h, i).wait_send()
 
     def b_copy(h, k):
         return pltpu.make_async_remote_copy(
@@ -320,97 +336,131 @@
         )
 
     def finish_a(h):
-        @pl.loop(0, 8)
-        def _(n):
-            k = (n + z + 1) & 7
-            for xs in range(2):
-                mine = jnp.logical_and(core == xhi, jnp.logical_and(xhi == xs, k == kz))
-
-                @pl.when(jnp.logical_not(mine))
-                def _():
-                    a_arrival(h, xs, k).wait_recv()
+        for d in (1, 2, 3, 4, 5, 6, 7, 0):
+            k = z ^ d
+            a_arrival(h, 1 - xhi, k).wait_recv()
+
+            @pl.when(jnp.logical_or(core != xhi, k != kz))
+            def _():
+                a_arrival(h, xhi, k).wait_recv()
 
             pb[h, k] = ra[h, 0, k] + ra[h, 1, k]
-
-            @pl.when(k != z)
-            def _():
+            if d:
                 b_copy(h, k).start()
 
     def finish_b(h):
-        rb[h, z] = pb[h, z]
-
-        @pl.loop(0, 8)
-        def _(zs):
-            @pl.when(zs != z)
-            def _():
-                b_arrival(h, zs).wait_recv()
-
-        total = rb[h, 0]
-        for zs in range(1, 8):
-            total = total + rb[h, zs]
+        total = pb[h, z]
+        for d in range(1, 8):
+            b_arrival(h, z ^ d).wait_recv()
+            total = total + rb[h, z ^ d]
         out_ref[:, 0, 4 * h : 4 * h + 4, :] = total[:, :4]
         out_ref[:, 1, 4 * h : 4 * h + 4, :] = total[:, 4:]
 
+    def end_b(h):
+        for d in range(1, 8):
+            b_copy(h, z ^ d).wait_send()
+
+    def end_strips():
+        for u in range(2 * NT):
+            d2d(u).wait_send()
+            for k in range(3):
+                for gi in range(3):
+                    exchange(u, k, gi).wait_send()
+
+    def first_product():
+        x_copy(0).wait()
+        split_x(0)
+        matmul(0)
+        wait_barrier()
+        d2d(0).start()
+
+    def product(u):
+        if 0 < u < NT:
+            x_copy(u).wait()
+            split_x(u)
+        if u == NT:
+            gen_t(1)
+        matmul(u)
+        d2d(u).start()
+
+    def last_tables():
+        strip_copy().wait()
+        gen_cols()
+
+    steps = {"d": finish_d2d, "c": columns, "a": finish_a, "s": start_a, "m": product}
+    gen_slots()
+    strip_copy().start()
     gen_u()
     gen_t(0)
-    slots = 2 * NT
-    for v in range(slots + 4):
-        if v < NT:
-            x_copy(v).wait()
-            split_x(v)
-        if v == 1:
-            gen_cols()
-        if v == NT:
-            gen_t(1)
-        if v < slots:
-            matmul(v)
-            if v == 0:
-                wait_barrier()
-            d2d(v).start()
-        if 0 <= v - 1 < slots:
-            finish_d2d(v - 1)
-        for k in range(3):
-            if 0 <= v - 2 - k < slots:
-                finish_exchange(v - 2 - k, k)
-        if 0 <= v - 4 < slots:
-            columns(v - 4)
-            if v - 4 == NT - 1:
-                start_a(0)
-        if v == slots + 1:
-            finish_a(0)
-    start_a(1)
-    finish_b(0)
+    first_product()
+    for kind, u in plan():
+        if kind == "g":
+            last_tables()
+        elif kind == "e":
+            finish_exchange(*u)
+        elif kind == "b":
+            finish_b(u)
+        else:
+            steps[kind](u)
+    end_strips()
+    end_a(0)
+    end_b(0)
     finish_a(1)
+    end_a(1)
     finish_b(1)
-
-    for u in range(slots):
-        d2d(u).wait_send()
-        for k in range(3):
-            for gi in range(3):
-                exchange(u, k, gi).wait_send()
-
-    @pl.loop(0, 16)
-    def _(a):
-        for h in range(2):
-
-            @pl.when(a_remote(a))
-            def _():
-                a_copy(h, a).wait_send()
-
-    @pl.loop(0, 8)
-    def _(k):
-        for h in range(2):
-
-            @pl.when(k != z)
-            def _():
-                b_copy(h, k).wait_send()
+    end_b(1)
+
+
+def plan():
+    wire = {"d": 1.6, 0: 3.0, 1: 2.6, 2: 2.3}
+    now, out, pending, ready = 0.0, [], [("d", 0, 1.6)], []
+    todo = list(range(1, 2 * NT))
+    tables = False
+    while todo or pending or ready:
+        due = sorted((t, k, u) for k, u, t in pending if t <= now)
+        if due:
+            t, kind, u = due[0]
+            pending.remove((kind, u, t))
+            out.append((kind, u))
+            if kind == "d":
+                pending.append(("e", (u, 0), now + 0.1 + wire[0]))
+            elif kind == "e":
+                u, k = u
+                if k < 2:
+                    pending.append(("e", (u, k + 1), now + 0.1 + wire[k + 1]))
+                else:
+                    ready.append(u)
+            elif kind == "a":
+                pending.append(("b", u, now + 6.5))
+            now += 0.1
+        elif ready:
+            if not tables:
+                tables = True
+                out.append(("g", 0))
+                now += 1.5
+            u = ready.pop(0)
+            out.append(("c", u))
+            now += 0.35
+            if u % NT == NT - 1:
+                out.append(("s", u // NT))
+                now += 0.25
+                if u // NT == 0:
+                    pending.append(("a", 0, now + 5.5))
+        elif todo:
+            u = todo.pop(0)
+            out.append(("m", u))
+            now += 1.75 + (0.3 if u < NT else 0) + (1.05 if u == NT else 0)
+            pending.append(("d", u, now + wire["d"]))
+        else:
+            if not tables:
+                tables = True
+                out.append(("g", 0))
+                now += 1.5
+            now = max(now, min(t for _, _, t in pending))
+    return out
 
 
 def per_device(facets, row_off, col_off, strip_offset, subgrid_strip, subgrid_column, subgrid_slot):
-    ids = jnp.arange(SLOTS, dtype=jnp.int32)
-    hit = subgrid_slot[None, :] == ids[:, None]
-    strip_of = jnp.sum(jnp.where(hit, subgrid_strip[None, :], 0), axis=1)
-    col_of = jnp.sum(jnp.where(hit, subgrid_column[None, :], 0), axis=1, keepdims=True)
     smem = pl.BlockSpec(memory_space=pltpu.SMEM)
     vmem = pl.BlockSpec(memory_space=pltpu.VMEM)
     dma = pltpu.SemaphoreType.DMA
@@ -418,9 +468,12 @@
     return pl.pallas_call(
         kernel,
         out_shape=jax.ShapeDtypeStruct((3, 2, 8, M), f32),
-        in_specs=[pl.BlockSpec(memory_space=pl.ANY), smem, smem, smem, smem, vmem],
+        in_specs=[pl.BlockSpec(memory_space=pl.ANY)] + [smem] * 6,
         out_specs=vmem,
         scratch_shapes=[
+            pltpu.VMEM((1, 128), jnp.int32),
+            pltpu.SMEM((1, 128), jnp.int32),
+            pltpu.VMEM((SLOTS, 1), jnp.int32),
             pltpu.VMEM((NT, 2, F, CW), f32),
             pltpu.VMEM((NT, 2 * F, CW), bf16),
             pltpu.VMEM((NT, 2 * F, CW), bf16),
@@ -445,6 +498,7 @@
             pltpu.VMEM((2, 8, 3, 8, M), f32),
             pltpu.VMEM((2, 8, 3, 8, M), f32),
             dma((NT,)),
+            dma((1,)),
             dma((u,)),
             dma((u,)),
             dma((u, 3, 3)),
@@ -455,10 +509,10 @@
             dma((2, 8)),
         ],
         compiler_params=pltpu.CompilerParams(
-            collective_id=0, has_side_effects=True, vmem_limit_bytes=60 * 1024 * 1024
+            collective_id=0, has_side_effects=True, vmem_limit_bytes=56 * 1024 * 1024
         ),
         name="facet_to_subgrid",
-    )(facets, row_off, col_off, strip_offset, strip_of, col_of)
+    )(facets, row_off, col_off, strip_offset, subgrid_strip, subgrid_column, subgrid_slot)
 
 
 def solution(mesh):

time: 74.5 us -> 60.7 us (0.81)
  Pallas kernels: 69.6 us -> 57.7 us
  other arithmetic: 1.34 us -> 0 us
    pallas_call x1, Pallas kernels: 69.6 us -> 57.7 us  [per_device(): pl.pallas_call(kernel, out_shape=jax.ShapeDtypeStruct((3, 2, 8, M), f32),...]
    reduce_sum x1 -> x0, other arithmetic: 1.34 us -> none  [per_device(): jnp.sum(jnp.where(hit, subgrid_column[None, :], 0), axis=1, keepdims=True)]
where the time goes in v1:
time: 60.7 us; the launch traced here: 60.3 us
  Pallas kernels  57.7 us (95%)
  local copies, waits for them, and re-layouts  1.35 us (2%)
  between operations  1.31 us (2%)
    pallas_call x1, Pallas kernels, per_device(): pl.pallas_call(kernel, out_shape=jax.ShapeDtypeStruct((3, 2, 8, M), f32),...  57.7 us
    unnamed x1, local copies, waits for them, and re-layouts  1.35 us

profile of v1, /device:TPU:1, one launch (start us, length us, event | category | flops | bytes accessed | tf_op | source)
XLA Modules:
  0.0 60.3 jit_solution(2472358402405554460)
XLA Ops:
  1.3 57.7 %facet_to_subgrid.1 = f32[3,2,8,128]{3,2,1,0:T(8,128)} custom-call(f32[2,1024,1024]{2,1,0:T(8,128)} %x_hbm.1, s32[1]{0:T(128)S(6)} %copy.9.roff, s32[1]{0:T(128)S(6)} %copy.10.coff, s32[4]{0:T(128)} %soff.1, s32[48]{0:T(128)} %g_strip.1, s32[48]{0:T(128)} %g_column.1, s32[48]{0:T(128)} %g_slot.1), custom_call_target="tpu_custom_call" | custom-call | tf_op jit(solution)/shard_map/facet_to_subgrid/pallas_call | solution.py:468
  59.0 1.3 %copy.11 = f32[3,2,8,128]{3,2,1,0:T(8,128)} copy(f32[3,2,8,128]{3,2,1,0:T(8,128)} %facet_to_subgrid.1) | data formatting | bytes 49152

commit v2 on v1

--- a/solution.py
+++ b/solution.py
@@ -67,10 +67,18 @@
 
 
 def kernel(
-    x_hbm, roff, coff, soff, g_strip, g_column, g_slot, out_ref,
+    x_hbm, *rest,
+):
+    scalars, (out_ref, *rest) = rest[:6], rest[6:]
+    (roff, coff, soff, g_strip, g_column, g_slot), rest = rest[:6], rest[6:]
+    body(x_hbm, scalars, roff, coff, soff, g_strip, g_column, g_slot, out_ref, *rest)
+
+
+def body(
+    x_hbm, scalars, roff, coff, soff, g_strip, g_column, g_slot, out_ref,
     strip_row, strip_of, col_of, xf, xh, xl, th, tl, ut, vt, s, rd, r0, r1, r2,
     fb, ph, eh, el, ah, al, gacc, g, ra, pb, rb,
-    x_sem, st_sem, d_ssem, d_rsem, e_ssem, e_rsem, a_ssem, a_rsem, b_ssem, b_rsem,
+    x_sem, st_sem, in_sem, d_ssem, d_rsem, e_ssem, e_rsem, a_ssem, a_rsem, b_ssem, b_rsem,
 ):
     i = lax.axis_index("frow")
     j = lax.axis_index("fcol")
@@ -88,6 +96,12 @@
             x_hbm.at[:, :, pl.ds(t * CW, CW)], xf.at[t], x_sem.at[t]
         )
 
+    def scalar_copies():
+        for n, (src, dst) in enumerate(zip(scalars, (roff, coff, soff, g_strip, g_column, g_slot))):
+            yield pltpu.make_async_copy(src, dst, in_sem.at[n])
+
+    for copy in scalar_copies():
+        copy.start()
     for t in range(NT):
         x_copy(t).start()
 
@@ -139,7 +153,7 @@
             ut[0, :, b * 256 : (b + 1) * 256] = cos
             ut[1, :, b * 256 : (b + 1) * 256] = sin
 
-    def gen_t(h):
+    def gen_v(h):
         r = iota((8, 1), 0)
         jj = iota((1, F), 1)
         m = ((r & 3) + 4 * h) * (roff[0] + jj) + (r >> 2) * (N // 4)
@@ -148,12 +162,13 @@
         vt[0] = w * cos
         vt[1] = w * sin
 
+    def gen_t(h, blocks):
         for b in range(4):
             cols = slice(b * 256, (b + 1) * 256)
             right = slice(F + b * 256, F + (b + 1) * 256)
             vr = vt[0, :, cols]
             vi = vt[1, :, cols]
-            for kb in range(16):
+            for kb in blocks:
                 left_t, right_t = [], []
                 for c in range(4):
                     q = kb * 4 + c
@@ -169,14 +184,11 @@
                 tl[h, kb, :, right] = lo
 
     def split_x(t):
-        @pl.loop(0, 8)
-        def _(b):
-            rows = pl.ds(pl.multiple_of(b * 128, 128), 128)
-            for part in range(2):
-                hi, lo = split(xf[t, part, rows, :])
-                dst = pl.ds(pl.multiple_of(part * F + b * 128, 128), 128)
-                xh[t, dst, :] = hi
-                xl[t, dst, :] = lo
+        for part in range(2):
+            for b in range(0, F, 128):
+                hi, lo = split(xf[t, part, b : b + 128, :])
+                xh[t, part * F + b : part * F + b + 128, :] = hi
+                xl[t, part * F + b : part * F + b + 128, :] = lo
 
     def gen_cols():
         for b in range(4):
@@ -196,14 +208,22 @@
             eh[rows, :] = hi
             el[rows, :] = lo
 
-    def matmul(u):
+    def matmul(u, half):
         h, t = divmod(u, NT)
-        for half in range(2):
-            rows = slice(8 * half, 8 * half + 8)
+        rows = slice(8 * half, 8 * half + 8)
+        out = dot3(
+            th[h, rows].reshape(256, 2 * F), tl[h, rows].reshape(256, 2 * F), xh[t], xl[t]
+        )
+        s[u, half] = out.reshape(2, 2, 2, 4, 8, CW)
+
+    def matmul_of(u, owner):
+        h, t = divmod(u, NT)
+        for x in range(2):
+            rows = pl.ds(8 * owner + 4 * x, 4)
             out = dot3(
-                th[h, rows].reshape(256, 2 * F), tl[h, rows].reshape(256, 2 * F), xh[t], xl[t]
+                th[h, rows].reshape(128, 2 * F), tl[h, rows].reshape(128, 2 * F), xh[t], xl[t]
             )
-            s[u, half] = out.reshape(2, 2, 2, 4, 8, CW)
+            s[u, owner, x] = out.reshape(2, 2, 4, 8, CW)
 
     def d2d(u):
         return pltpu.make_async_remote_copy(
@@ -367,110 +387,91 @@
                 for gi in range(3):
                     exchange(u, k, gi).wait_send()
 
-    def first_product():
-        x_copy(0).wait()
-        split_x(0)
-        matmul(0)
-        wait_barrier()
-        d2d(0).start()
+    last = 2 * NT - 1
+    cuts = {1: range(0, 6), 2: range(6, 11), 3: range(11, 16)}
 
     def product(u):
-        if 0 < u < NT:
-            x_copy(u).wait()
-            split_x(u)
-        if u == NT:
-            gen_t(1)
-        matmul(u)
-        d2d(u).start()
-
-    def last_tables():
-        strip_copy().wait()
-        gen_cols()
-
-    steps = {"d": finish_d2d, "c": columns, "a": finish_a, "s": start_a, "m": product}
+        if u + 1 < NT:
+            x_copy(u + 1).wait()
+            split_x(u + 1)
+        if u == 1:
+            gen_v(1)
+        if u in cuts:
+            gen_t(1, cuts[u])
+        if u < last:
+            matmul(u, 0)
+            matmul(u, 1)
+            if u == 0:
+                wait_barrier()
+            d2d(u).start()
+        else:
+            matmul_of(u, 1 - core)
+            d2d(u).start()
+            matmul_of(u, core)
+
+    for copy in scalar_copies():
+        copy.wait()
     gen_slots()
     strip_copy().start()
     gen_u()
-    gen_t(0)
-    first_product()
-    for kind, u in plan():
-        if kind == "g":
-            last_tables()
+    gen_v(0)
+    gen_t(0, range(16))
+    x_copy(0).wait()
+    split_x(0)
+    for kind, *at in PLAN:
+        if kind == "m":
+            product(*at)
+        elif kind == "d":
+            finish_d2d(*at)
         elif kind == "e":
-            finish_exchange(*u)
+            finish_exchange(*at)
+        elif kind == "g":
+            strip_copy().wait()
+            gen_cols()
+        elif kind == "c":
+            columns(*at)
+        elif kind == "s":
+            start_a(*at)
+        elif kind == "w":
+            end_strips()
+        elif kind == "a":
+            finish_a(*at)
+        elif kind == "x":
+            end_a(*at)
         elif kind == "b":
-            finish_b(u)
-        else:
-            steps[kind](u)
-    end_strips()
-    end_a(0)
-    end_b(0)
-    finish_a(1)
-    end_a(1)
-    finish_b(1)
-    end_b(1)
-
-
-def plan():
-    wire = {"d": 1.6, 0: 3.0, 1: 2.6, 2: 2.3}
-    now, out, pending, ready = 0.0, [], [("d", 0, 1.6)], []
-    todo = list(range(1, 2 * NT))
-    tables = False
-    while todo or pending or ready:
-        due = sorted((t, k, u) for k, u, t in pending if t <= now)
-        if due:
-            t, kind, u = due[0]
-            pending.remove((kind, u, t))
-            out.append((kind, u))
-            if kind == "d":
-                pending.append(("e", (u, 0), now + 0.1 + wire[0]))
-            elif kind == "e":
-                u, k = u
-                if k < 2:
-                    pending.append(("e", (u, k + 1), now + 0.1 + wire[k + 1]))
-                else:
-                    ready.append(u)
-            elif kind == "a":
-                pending.append(("b", u, now + 6.5))
-            now += 0.1
-        elif ready:
-            if not tables:
-                tables = True
-                out.append(("g", 0))
-                now += 1.5
-            u = ready.pop(0)
-            out.append(("c", u))
-            now += 0.35
-            if u % NT == NT - 1:
-                out.append(("s", u // NT))
-                now += 0.25
-                if u // NT == 0:
-                    pending.append(("a", 0, now + 5.5))
-        elif todo:
-            u = todo.pop(0)
-            out.append(("m", u))
-            now += 1.75 + (0.3 if u < NT else 0) + (1.05 if u == NT else 0)
-            pending.append(("d", u, now + wire["d"]))
-        else:
-            if not tables:
-                tables = True
-                out.append(("g", 0))
-                now += 1.5
-            now = max(now, min(t for _, _, t in pending))
-    return out
+            finish_b(*at)
+        elif kind == "y":
+            end_b(*at)
+
+
+PLAN = (
+    ("m", 0),
+    ("m", 1), ("d", 0),
+    ("m", 2), ("d", 1),
+    ("m", 3), ("e", 0, 0), ("d", 2),
+    ("m", 4), ("e", 1, 0), ("d", 3), ("e", 0, 1),
+    ("m", 5), ("e", 2, 0), ("d", 4), ("e", 1, 1),
+    ("m", 6), ("e", 3, 0), ("d", 5), ("e", 0, 2), ("e", 2, 1),
+    ("m", 7), ("e", 4, 0), ("d", 6), ("e", 1, 2), ("e", 3, 1), ("e", 5, 0), ("d", 7),
+    ("e", 2, 2), ("g",), ("e", 4, 1), ("e", 6, 0), ("e", 3, 2), ("e", 5, 1), ("c", 0), ("c", 1), ("c", 2),
+    ("e", 7, 0), ("e", 4, 2), ("e", 6, 1), ("e", 5, 2), ("c", 3), ("c", 4), ("c", 5),
+    ("e", 7, 1), ("s", 0), ("e", 6, 2), ("c", 6),
+    ("e", 7, 2), ("c", 7), ("s", 1), ("w",),
+    ("a", 0), ("x", 0), ("a", 1), ("x", 1), ("b", 0), ("y", 0), ("b", 1), ("y", 1),
+)
 
 
 def per_device(facets, row_off, col_off, strip_offset, subgrid_strip, subgrid_column, subgrid_slot):
-    smem = pl.BlockSpec(memory_space=pltpu.SMEM)
     vmem = pl.BlockSpec(memory_space=pltpu.VMEM)
     dma = pltpu.SemaphoreType.DMA
     u = 2 * NT
     return pl.pallas_call(
         kernel,
         out_shape=jax.ShapeDtypeStruct((3, 2, 8, M), f32),
-        in_specs=[pl.BlockSpec(memory_space=pl.ANY)] + [smem] * 6,
+        in_specs=[pl.BlockSpec(memory_space=pl.ANY)] * 7,
         out_specs=vmem,
         scratch_shapes=[
+            *(pltpu.SMEM((n,), jnp.int32) for n in (1, 1, 4, SLOTS, SLOTS, SLOTS)),
             pltpu.VMEM((1, 128), jnp.int32),
             pltpu.SMEM((1, 128), jnp.int32),
             pltpu.VMEM((SLOTS, 1), jnp.int32),
@@ -499,6 +500,7 @@
             pltpu.VMEM((2, 8, 3, 8, M), f32),
             dma((NT,)),
             dma((1,)),
+            dma((6,)),
             dma((u,)),
             dma((u,)),
             dma((u, 3, 3)),

time: 60.7 us -> 60 us (0.988)
  no operation moved by 1% of the time
where the time goes in v2:
time: 60 us; the launch traced here: 59.8 us
  Pallas kernels  57.2 us (95%)
  local copies, waits for them, and re-layouts  1.35 us (2%)
  between operations  1.31 us (2%)
    pallas_call x1, Pallas kernels, per_device(): pl.pallas_call(kernel, out_shape=jax.ShapeDtypeStruct((3, 2, 8, M), f32),...  57.2 us
    unnamed x1, local copies, waits for them, and re-layouts  1.35 us

profile of v2, /device:TPU:1, one launch (start us, length us, event | category | flops | bytes accessed | tf_op | source)
XLA Modules:
  0.0 59.8 jit_solution(14327975828094626888)
XLA Ops:
  1.3 57.2 %facet_to_subgrid.1 = f32[3,2,8,128]{3,2,1,0:T(8,128)} custom-call(f32[2,1024,1024]{2,1,0:T(8,128)} %x_hbm.1, s32[1]{0:T(128)S(6)} %copy.9.rest_0_, s32[1]{0:T(128)S(6)} %copy.10.rest_1_, s32[4]{0:T(128)} %rest_2_.1, s32[48]{0:T(128)} %rest_3_.1, s32[48]{0:T(128)} %rest_4_.1, s32[48]{0:T(128)} %rest_5_.1), custom_call_target="tpu_custom_call" | custom-call | tf_op jit(solution)/shard_map/facet_to_subgrid/pallas_call | solution.py:468
  58.5 1.3 %copy.11 = f32[3,2,8,128]{3,2,1,0:T(8,128)} copy(f32[3,2,8,128]{3,2,1,0:T(8,128)} %facet_to_subgrid.1) | data formatting | bytes 49152

commit v3 on v2

--- a/solution.py
+++ b/solution.py
@@ -14,12 +14,17 @@
 SLOTS = 48
 CW = 256
 NT = F // CW
+LAST = 2 * NT - 1
 f32 = jnp.float32
 bf16 = jnp.bfloat16
 MESH = pl.DeviceIdType.MESH
 
 FLIP = (8, 2, 6)
 ORDERS = ((0, 1, 2), (1, 2, 0), (2, 0, 1))
+
+
+def flip_of(d):
+    return (8 if d & 4 else 0) ^ (2 if d & 2 else 0) ^ (6 if d & 1 else 0)
 
 
 def groups_of(u):
@@ -76,9 +81,9 @@
 
 def body(
     x_hbm, scalars, roff, coff, soff, g_strip, g_column, g_slot, out_ref,
-    strip_row, strip_of, col_of, xf, xh, xl, th, tl, ut, vt, s, rd, r0, r1, r2,
+    strip_row, strip_of, col_of, xf, xh, xl, th, tl, ut, vt, wt, s, rd, r0, r1, r2, r7,
     fb, ph, eh, el, ah, al, gacc, g, ra, pb, rb,
-    x_sem, st_sem, in_sem, d_ssem, d_rsem, e_ssem, e_rsem, a_ssem, a_rsem, b_ssem, b_rsem,
+    x_sem, st_sem, in_sem, d_ssem, d_rsem, e_ssem, e_rsem, f_ssem, f_rsem, a_ssem, a_rsem, b_ssem, b_rsem,
 ):
     i = lax.axis_index("frow")
     j = lax.axis_index("fcol")
@@ -110,7 +115,7 @@
     def hello(fr, fc):
         pl.semaphore_signal(barrier, inc=1, device_id=(fr, fc), device_id_type=MESH)
 
-    for flip in (1, *FLIP):
+    for flip in (1, *(flip_of(d) for d in range(1, 8))):
         hello(i ^ flip, j)
 
     for d in range(1, 16):
@@ -124,7 +129,7 @@
         hello(i, (z ^ d) * 2 + xhi)
 
     def wait_barrier():
-        pl.semaphore_wait(barrier, 27 - (1 - (core ^ xhi)))
+        pl.semaphore_wait(barrier, 31 - (1 - (core ^ xhi)))
 
     def gen_slots():
         lane = iota((1, 128), 1)
@@ -156,39 +161,42 @@
     def gen_v(h):
         r = iota((8, 1), 0)
         jj = iota((1, F), 1)
-        m = ((r & 3) + 4 * h) * (roff[0] + jj) + (r >> 2) * (N // 4)
-        cos, sin = cos_sin(m & MASK)
+        cos, sin = cos_sin((((r & 3) + 4 * h) * (roff[0] + jj)) & MASK)
         w = window(jj)
         vt[0] = w * cos
         vt[1] = w * sin
 
-    def gen_t(h, blocks):
+    def gen_t(h):
+        first = iota((8, 1), 0) < 4
         for b in range(4):
             cols = slice(b * 256, (b + 1) * 256)
-            right = slice(F + b * 256, F + (b + 1) * 256)
             vr = vt[0, :, cols]
             vi = vt[1, :, cols]
-            for kb in blocks:
-                left_t, right_t = [], []
-                for c in range(4):
+            for kb in range(16):
+                tiles = [[], [], []]
+                for c in (0, 2):
                     q = kb * 4 + c
-                    ur = ut[0, q : q + 1, cols]
-                    ui = ut[1, q : q + 1, cols]
-                    left_t.append(ur * vr - ui * vi)
-                    right_t.append(ui * vr + ur * vi)
-                hi, lo = split(jnp.concatenate(left_t, 0))
-                th[h, kb, :, cols] = hi
-                tl[h, kb, :, cols] = lo
-                hi, lo = split(jnp.concatenate(right_t, 0))
-                th[h, kb, :, right] = hi
-                tl[h, kb, :, right] = lo
+                    ur = jnp.where(first, ut[0, q : q + 1, cols], ut[0, q + 1 : q + 2, cols])
+                    ui = jnp.where(first, ut[1, q : q + 1, cols], ut[1, q + 1 : q + 2, cols])
+                    re = ur * vr - ui * vi
+                    im = -(ui * vr + ur * vi)
+                    for tile, value in zip(tiles, (re, re + im, im - re)):
+                        tile.append(value)
+                for p in range(3):
+                    hi, lo = split(jnp.concatenate(tiles[p], 0))
+                    th[h, p, kb, :, cols] = hi
+                    tl[h, p, kb, :, cols] = lo
 
     def split_x(t):
-        for part in range(2):
-            for b in range(0, F, 128):
-                hi, lo = split(xf[t, part, b : b + 128, :])
-                xh[t, part * F + b : part * F + b + 128, :] = hi
-                xl[t, part * F + b : part * F + b + 128, :] = lo
+        @pl.loop(0, 8)
+        def _(b):
+            rows = pl.ds(pl.multiple_of(b * 128, 128), 128)
+            re = xf[t, 0, rows, :]
+            im = xf[t, 1, rows, :]
+            for p, value in enumerate((re + im, im, re)):
+                hi, lo = split(value)
+                xh[t, p, rows, :] = hi
+                xl[t, p, rows, :] = lo
 
     def gen_cols():
         for b in range(4):
@@ -198,32 +206,42 @@
             ph[0, :, b * 256 : (b + 1) * 256] = w * cos
             ph[1, :, b * 256 : (b + 1) * 256] = -(w * sin)
 
-        @pl.loop(0, 32)
+        lane = iota((1, M), 1)
+        cos, sin = cos_sin((lane * (coff[0] + 8 * iota((F // 8, 1), 0))) & MASK)
+        wt[0] = cos
+        wt[1] = sin
+        c1, s1 = cos_sin((lane * iota((8, 1), 0)) & MASK)
+
+        @pl.loop(0, 16)
         def _(b):
-            n = b * 32 + iota((32, 1), 0)
-            m = (iota((1, M), 1) * (coff[0] + n)) & MASK
-            cos, sin = cos_sin(m)
-            hi, lo = split(jnp.concatenate([cos, -sin], 1))
-            rows = pl.ds(pl.multiple_of(b * 32, 32), 32)
-            eh[rows, :] = hi
-            el[rows, :] = lo
+            eight = pl.ds(pl.multiple_of(b * 8, 8), 8)
+            wc = wt[0, eight, :]
+            ws = wt[1, eight, :]
+            for k in range(0, 8, 2):
+                pair = []
+                for n in (k, k + 1):
+                    c0 = wc[n : n + 1]
+                    s0 = ws[n : n + 1]
+                    pair.append(jnp.concatenate([c0 * c1 - s0 * s1, -(s0 * c1 + c0 * s1)], 1))
+                hi, lo = split(jnp.concatenate(pair, 0))
+                rows = pl.ds(pl.multiple_of(b * 64 + k * 8, 16), 16)
+                eh[rows, :] = hi
+                el[rows, :] = lo
 
     def matmul(u, half):
         h, t = divmod(u, NT)
-        rows = slice(8 * half, 8 * half + 8)
-        out = dot3(
-            th[h, rows].reshape(256, 2 * F), tl[h, rows].reshape(256, 2 * F), xh[t], xl[t]
-        )
-        s[u, half] = out.reshape(2, 2, 2, 4, 8, CW)
-
-    def matmul_of(u, owner):
-        h, t = divmod(u, NT)
-        for x in range(2):
-            rows = pl.ds(8 * owner + 4 * x, 4)
-            out = dot3(
-                th[h, rows].reshape(128, 2 * F), tl[h, rows].reshape(128, 2 * F), xh[t], xl[t]
+        rows = pl.ds(8 * half, 8)
+        k1, k2, k3 = (
+            dot3(
+                th[h, p, rows].reshape(128, F), tl[h, p, rows].reshape(128, F), xh[t, p], xl[t, p]
             )
-            s[u, owner, x] = out.reshape(2, 2, 4, 8, CW)
+            for p in range(3)
+        )
+        re = (k1 - k2).reshape(2, 2, 2, 2, 8, CW)
+        im = (k1 + k3).reshape(2, 2, 2, 2, 8, CW)
+        for pair in range(2):
+            s[u, half, :, :, :, 2 * pair] = re[:, :, :, pair]
+            s[u, half, :, :, :, 2 * pair + 1] = im[:, :, :, pair]
 
     def d2d(u):
         return pltpu.make_async_remote_copy(
@@ -256,8 +274,30 @@
     def finish_d2d(u):
         d2d(u).wait_recv()
         s[u, core] += rd[u]
-        for gi in range(3):
-            exchange(u, 0, gi).start()
+        if u == LAST:
+            for d in range(1, 8):
+                direct(d).start()
+        else:
+            for gi in range(3):
+                exchange(u, 0, gi).start()
+
+    def direct(d):
+        to = (own[0] ^ (d >> 2), own[1] ^ ((d >> 1) & 1), own[2] ^ (d & 1))
+        return pltpu.make_async_remote_copy(
+            src_ref=s.at[(LAST, core, *to)],
+            dst_ref=r7.at[d],
+            send_sem=f_ssem.at[d],
+            recv_sem=f_rsem.at[d],
+            device_id=(i ^ flip_of(d), j),
+            device_id_type=MESH,
+        )
+
+    def finish_direct():
+        total = s[(LAST, core, *own)]
+        for d in range(1, 8):
+            direct(d).wait_recv()
+            total = total + r7[d]
+        s[(LAST, core, *own)] = total
 
     def finish_exchange(u, k):
         for gi, (order, c0, n) in enumerate(groups_of(u)):
@@ -272,10 +312,13 @@
     def columns(u):
         h, t = divmod(u, NT)
         cols = slice(t * CW, (t + 1) * CW)
-        for c in range(4):
-            tile = s[u, core, own[0], own[1], own[2], c]
-            fb[0, c] = tile
-            fb[1, c] = jnp.concatenate([tile[4:], tile[:4]], 0) * sign
+        for pair in range(2):
+            re = s[u, core, own[0], own[1], own[2], 2 * pair]
+            im = s[u, core, own[0], own[1], own[2], 2 * pair + 1]
+            fb[0, 2 * pair] = jnp.concatenate([re[:4], im[:4]], 0)
+            fb[1, 2 * pair] = jnp.concatenate([-im[:4], re[:4]], 0)
+            fb[0, 2 * pair + 1] = jnp.concatenate([re[4:], im[4:]], 0)
+            fb[1, 2 * pair + 1] = jnp.concatenate([-im[4:], re[4:]], 0)
         for q0 in range(0, SLOTS, 4):
             tiles = []
             for q in range(q0, q0 + 4):
@@ -381,33 +424,28 @@
             b_copy(h, z ^ d).wait_send()
 
     def end_strips():
+        for d in range(1, 8):
+            direct(d).wait_send()
         for u in range(2 * NT):
             d2d(u).wait_send()
-            for k in range(3):
+            for k in range(3 if u < LAST else 0):
                 for gi in range(3):
                     exchange(u, k, gi).wait_send()
 
-    last = 2 * NT - 1
-    cuts = {1: range(0, 6), 2: range(6, 11), 3: range(11, 16)}
-
     def product(u):
-        if u + 1 < NT:
-            x_copy(u + 1).wait()
-            split_x(u + 1)
-        if u == 1:
-            gen_v(1)
-        if u in cuts:
-            gen_t(1, cuts[u])
-        if u < last:
+        if u < NT:
+            x_copy(u).wait()
+            split_x(u)
+        if u < LAST:
             matmul(u, 0)
             matmul(u, 1)
             if u == 0:
                 wait_barrier()
             d2d(u).start()
         else:
-            matmul_of(u, 1 - core)
+            matmul(u, 1 - core)
             d2d(u).start()
-            matmul_of(u, core)
+            matmul(u, core)
 
     for copy in scalar_copies():
         copy.wait()
@@ -415,9 +453,7 @@
     strip_copy().start()
     gen_u()
     gen_v(0)
-    gen_t(0, range(16))
-    x_copy(0).wait()
-    split_x(0)
+    gen_t(0)
     for kind, *at in PLAN:
         if kind == "m":
             product(*at)
@@ -425,6 +461,11 @@
             finish_d2d(*at)
         elif kind == "e":
             finish_exchange(*at)
+        elif kind == "f":
+            finish_direct()
+        elif kind == "t":
+            gen_v(1)
+            gen_t(1)
         elif kind == "g":
             strip_copy().wait()
             gen_cols()
@@ -448,15 +489,15 @@
     ("m", 0),
     ("m", 1), ("d", 0),
     ("m", 2), ("d", 1),
-    ("m", 3), ("e", 0, 0), ("d", 2),
-    ("m", 4), ("e", 1, 0), ("d", 3), ("e", 0, 1),
-    ("m", 5), ("e", 2, 0), ("d", 4), ("e", 1, 1),
-    ("m", 6), ("e", 3, 0), ("d", 5), ("e", 0, 2), ("e", 2, 1),
-    ("m", 7), ("e", 4, 0), ("d", 6), ("e", 1, 2), ("e", 3, 1), ("e", 5, 0), ("d", 7),
-    ("e", 2, 2), ("g",), ("e", 4, 1), ("e", 6, 0), ("e", 3, 2), ("e", 5, 1), ("c", 0), ("c", 1), ("c", 2),
-    ("e", 7, 0), ("e", 4, 2), ("e", 6, 1), ("e", 5, 2), ("c", 3), ("c", 4), ("c", 5),
-    ("e", 7, 1), ("s", 0), ("e", 6, 2), ("c", 6),
-    ("e", 7, 2), ("c", 7), ("s", 1), ("w",),
+    ("m", 3), ("d", 2), ("e", 0, 0),
+    ("t",), ("d", 3),
+    ("m", 4), ("e", 0, 1), ("e", 1, 0),
+    ("m", 5), ("d", 4), ("e", 2, 0),
+    ("m", 6), ("d", 5), ("e", 1, 1), ("e", 0, 2), ("e", 3, 0),
+    ("m", 7), ("d", 6), ("e", 2, 1), ("e", 4, 0), ("e", 1, 2), ("d", 7),
+    ("g",), ("e", 3, 1), ("e", 5, 0), ("e", 2, 2), ("c", 0), ("e", 4, 1), ("e", 6, 0), ("c", 1), ("e", 3, 2), ("c", 2),
+    ("e", 5, 1), ("e", 4, 2), ("c", 3), ("e", 6, 1), ("s", 0), ("c", 4), ("e", 5, 2), ("c", 5), ("e", 6, 2), ("c", 6), ("w",),
+    ("f",), ("c", 7), ("s", 1),
     ("a", 0), ("x", 0), ("a", 1), ("x", 1), ("b", 0), ("y", 0), ("b", 1), ("y", 1),
 )
 
@@ -476,17 +517,19 @@
             pltpu.SMEM((1, 128), jnp.int32),
             pltpu.VMEM((SLOTS, 1), jnp.int32),
             pltpu.VMEM((NT, 2, F, CW), f32),
-            pltpu.VMEM((NT, 2 * F, CW), bf16),
-            pltpu.VMEM((NT, 2 * F, CW), bf16),
-            pltpu.VMEM((2, 16, 32, 2 * F), bf16),
-            pltpu.VMEM((2, 16, 32, 2 * F), bf16),
+            pltpu.VMEM((NT, 3, F, CW), bf16),
+            pltpu.VMEM((NT, 3, F, CW), bf16),
+            pltpu.VMEM((2, 3, 16, 16, F), bf16),
+            pltpu.VMEM((2, 3, 16, 16, F), bf16),
             pltpu.VMEM((2, 64, F), f32),
             pltpu.VMEM((2, 8, F), f32),
+            pltpu.VMEM((2, F // 8, M), f32),
             pltpu.VMEM((u, 2, 2, 2, 2, 4, 8, CW), f32),
             pltpu.VMEM((u, 2, 2, 2, 4, 8, CW), f32),
             pltpu.VMEM((u, 2, 2, 4, 8, CW), f32),
             pltpu.VMEM((u, 2, 4, 8, CW), f32),
             pltpu.VMEM((u, 4, 8, CW), f32),
+            pltpu.VMEM((8, 4, 8, CW), f32),
             pltpu.VMEM((2, 4, 8, CW), f32),
             pltpu.VMEM((2, SLOTS, F), f32),
             pltpu.VMEM((F, 2 * M), bf16),
@@ -505,6 +548,8 @@
             dma((u,)),
             dma((u, 3, 3)),
             dma((u, 3, 3)),
+            dma((8,)),
+            dma((8,)),
             dma((2, 16)),
             dma((2, 2, 8)),
             dma((2, 8)),

time: 60 us -> 56.6 us (0.943)
  Pallas kernels: 57.2 us -> 53.8 us
    pallas_call x1, Pallas kernels: 57.2 us -> 53.8 us  [per_device(): pl.pallas_call(kernel, out_shape=jax.ShapeDtypeStruct((3, 2, 8, M), f32),...]
where the time goes in v3:
time: 56.6 us; the launch traced here: 56.4 us
  Pallas kernels  53.8 us (95%)
  local copies, waits for them, and re-layouts  1.35 us (2%)
  between operations  1.31 us (2%)
    pallas_call x1, Pallas kernels, per_device(): pl.pallas_call(kernel, out_shape=jax.ShapeDtypeStruct((3, 2, 8, M), f32),...  53.8 us
    unnamed x1, local copies, waits for them, and re-layouts  1.35 us

profile of v3, /device:TPU:1, one launch (start us, length us, event | category | flops | bytes accessed | tf_op | source)
XLA Modules:
  0.0 56.4 jit_solution(9765038871339647509)
XLA Ops:
  1.3 53.8 %facet_to_subgrid.1 = f32[3,2,8,128]{3,2,1,0:T(8,128)} custom-call(f32[2,1024,1024]{2,1,0:T(8,128)} %x_hbm.1, s32[1]{0:T(128)S(6)} %copy.9.rest_0_, s32[1]{0:T(128)S(6)} %copy.10.rest_1_, s32[4]{0:T(128)} %rest_2_.1, s32[48]{0:T(128)} %rest_3_.1, s32[48]{0:T(128)} %rest_4_.1, s32[48]{0:T(128)} %rest_5_.1), custom_call_target="tpu_custom_call" | custom-call | tf_op jit(solution)/shard_map/facet_to_subgrid/pallas_call | solution.py:509
  55.1 1.3 %copy.11 = f32[3,2,8,128]{3,2,1,0:T(8,128)} copy(f32[3,2,8,128]{3,2,1,0:T(8,128)} %facet_to_subgrid.1) | data formatting | bytes 49152

commit v4 on v3

--- a/solution.py
+++ b/solution.py
@@ -15,6 +15,7 @@
 CW = 256
 NT = F // CW
 LAST = 2 * NT - 1
+PIECES = (7, 6, 5, 3, 4, 2, 1)
 f32 = jnp.float32
 bf16 = jnp.bfloat16
 MESH = pl.DeviceIdType.MESH
@@ -274,30 +275,30 @@
     def finish_d2d(u):
         d2d(u).wait_recv()
         s[u, core] += rd[u]
-        if u == LAST:
-            for d in range(1, 8):
-                direct(d).start()
+        if u >= NT:
+            for d in PIECES:
+                direct(u, d).start()
         else:
             for gi in range(3):
                 exchange(u, 0, gi).start()
 
-    def direct(d):
+    def direct(u, d):
         to = (own[0] ^ (d >> 2), own[1] ^ ((d >> 1) & 1), own[2] ^ (d & 1))
         return pltpu.make_async_remote_copy(
-            src_ref=s.at[(LAST, core, *to)],
-            dst_ref=r7.at[d],
-            send_sem=f_ssem.at[d],
-            recv_sem=f_rsem.at[d],
+            src_ref=s.at[(u, core, *to)],
+            dst_ref=r7.at[u - NT, d],
+            send_sem=f_ssem.at[u - NT, d],
+            recv_sem=f_rsem.at[u - NT, d],
             device_id=(i ^ flip_of(d), j),
             device_id_type=MESH,
         )
 
-    def finish_direct():
-        total = s[(LAST, core, *own)]
-        for d in range(1, 8):
-            direct(d).wait_recv()
-            total = total + r7[d]
-        s[(LAST, core, *own)] = total
+    def finish_direct(u):
+        total = s[(u, core, *own)]
+        for d in PIECES:
+            direct(u, d).wait_recv()
+            total = total + r7[u - NT, d]
+        s[(u, core, *own)] = total
 
     def finish_exchange(u, k):
         for gi, (order, c0, n) in enumerate(groups_of(u)):
@@ -424,11 +425,11 @@
             b_copy(h, z ^ d).wait_send()
 
     def end_strips():
-        for d in range(1, 8):
-            direct(d).wait_send()
         for u in range(2 * NT):
             d2d(u).wait_send()
-            for k in range(3 if u < LAST else 0):
+            for d in PIECES if u >= NT else ():
+                direct(u, d).wait_send()
+            for k in range(3 if u < NT else 0):
                 for gi in range(3):
                     exchange(u, k, gi).wait_send()
 
@@ -462,7 +463,7 @@
         elif kind == "e":
             finish_exchange(*at)
         elif kind == "f":
-            finish_direct()
+            finish_direct(*at)
         elif kind == "t":
             gen_v(1)
             gen_t(1)
@@ -491,13 +492,12 @@
     ("m", 2), ("d", 1),
     ("m", 3), ("d", 2), ("e", 0, 0),
     ("t",), ("d", 3),
-    ("m", 4), ("e", 0, 1), ("e", 1, 0),
-    ("m", 5), ("d", 4), ("e", 2, 0),
-    ("m", 6), ("d", 5), ("e", 1, 1), ("e", 0, 2), ("e", 3, 0),
-    ("m", 7), ("d", 6), ("e", 2, 1), ("e", 4, 0), ("e", 1, 2), ("d", 7),
-    ("g",), ("e", 3, 1), ("e", 5, 0), ("e", 2, 2), ("c", 0), ("e", 4, 1), ("e", 6, 0), ("c", 1), ("e", 3, 2), ("c", 2),
-    ("e", 5, 1), ("e", 4, 2), ("c", 3), ("e", 6, 1), ("s", 0), ("c", 4), ("e", 5, 2), ("c", 5), ("e", 6, 2), ("c", 6), ("w",),
-    ("f",), ("c", 7), ("s", 1),
+    ("m", 4), ("e", 1, 0),
+    ("m", 5), ("d", 4), ("e", 0, 1), ("e", 2, 0), ("e", 3, 0),
+    ("m", 6), ("d", 5), ("e", 1, 1),
+    ("m", 7), ("d", 6), ("e", 2, 1), ("e", 3, 1), ("d", 7),
+    ("g",), ("e", 0, 2), ("c", 0), ("e", 1, 2), ("c", 1), ("e", 2, 2), ("c", 2), ("e", 3, 2), ("c", 3), ("s", 0),
+    ("f", 4), ("c", 4), ("f", 5), ("c", 5), ("f", 6), ("c", 6), ("w",), ("f", 7), ("c", 7), ("s", 1),
     ("a", 0), ("x", 0), ("a", 1), ("x", 1), ("b", 0), ("y", 0), ("b", 1), ("y", 1),
 )
 
@@ -526,10 +526,10 @@
             pltpu.VMEM((2, F // 8, M), f32),
             pltpu.VMEM((u, 2, 2, 2, 2, 4, 8, CW), f32),
             pltpu.VMEM((u, 2, 2, 2, 4, 8, CW), f32),
-            pltpu.VMEM((u, 2, 2, 4, 8, CW), f32),
-            pltpu.VMEM((u, 2, 4, 8, CW), f32),
-            pltpu.VMEM((u, 4, 8, CW), f32),
-            pltpu.VMEM((8, 4, 8, CW), f32),
+            pltpu.VMEM((NT, 2, 2, 4, 8, CW), f32),
+            pltpu.VMEM((NT, 2, 4, 8, CW), f32),
+            pltpu.VMEM((NT, 4, 8, CW), f32),
+            pltpu.VMEM((NT, 8, 4, 8, CW), f32),
             pltpu.VMEM((2, 4, 8, CW), f32),
             pltpu.VMEM((2, SLOTS, F), f32),
             pltpu.VMEM((F, 2 * M), bf16),
@@ -546,10 +546,10 @@
             dma((6,)),
             dma((u,)),
             dma((u,)),
-            dma((u, 3, 3)),
-            dma((u, 3, 3)),
-            dma((8,)),
-            dma((8,)),
+            dma((NT, 3, 3)),
+            dma((NT, 3, 3)),
+            dma((NT, 8)),
+            dma((NT, 8)),
             dma((2, 16)),
             dma((2, 2, 8)),
             dma((2, 8)),

time: 56.6 us -> 53.9 us (0.952)
  Pallas kernels: 53.8 us -> 51.1 us
    pallas_call x1, Pallas kernels: 53.8 us -> 51.1 us  [per_device(): pl.pallas_call(kernel, out_shape=jax.ShapeDtypeStruct((3, 2, 8, M), f32),...]
where the time goes in v4:
time: 53.9 us; the launch traced here: 53.7 us
  Pallas kernels  51.1 us (95%)
  local copies, waits for them, and re-layouts  1.35 us (3%)
  between operations  1.31 us (2%)
    pallas_call x1, Pallas kernels, per_device(): pl.pallas_call(kernel, out_shape=jax.ShapeDtypeStruct((3, 2, 8, M), f32),...  51.1 us
    unnamed x1, local copies, waits for them, and re-layouts  1.35 us

profile of v4, /device:TPU:1, one launch (start us, length us, event | category | flops | bytes accessed | tf_op | source)
XLA Modules:
  0.0 53.7 jit_solution(1393169093025676577)
XLA Ops:
  1.3 51.1 %facet_to_subgrid.1 = f32[3,2,8,128]{3,2,1,0:T(8,128)} custom-call(f32[2,1024,1024]{2,1,0:T(8,128)} %x_hbm.1, s32[1]{0:T(128)S(6)} %copy.9.rest_0_, s32[1]{0:T(128)S(6)} %copy.10.rest_1_, s32[4]{0:T(128)} %rest_2_.1, s32[48]{0:T(128)} %rest_3_.1, s32[48]{0:T(128)} %rest_4_.1, s32[48]{0:T(128)} %rest_5_.1), custom_call_target="tpu_custom_call" | custom-call | tf_op jit(solution)/shard_map/facet_to_subgrid/pallas_call | solution.py:509
  52.4 1.3 %copy.11 = f32[3,2,8,128]{3,2,1,0:T(8,128)} copy(f32[3,2,8,128]{3,2,1,0:T(8,128)} %facet_to_subgrid.1) | data formatting | bytes 49152

commit v5 on v4

--- a/solution.py
+++ b/solution.py
@@ -15,6 +15,7 @@
 CW = 256
 NT = F // CW
 LAST = 2 * NT - 1
+STEPPED = 3
 PIECES = (7, 6, 5, 3, 4, 2, 1)
 f32 = jnp.float32
 bf16 = jnp.bfloat16
@@ -275,7 +276,7 @@
     def finish_d2d(u):
         d2d(u).wait_recv()
         s[u, core] += rd[u]
-        if u >= NT:
+        if u >= STEPPED:
             for d in PIECES:
                 direct(u, d).start()
         else:
@@ -286,9 +287,9 @@
         to = (own[0] ^ (d >> 2), own[1] ^ ((d >> 1) & 1), own[2] ^ (d & 1))
         return pltpu.make_async_remote_copy(
             src_ref=s.at[(u, core, *to)],
-            dst_ref=r7.at[u - NT, d],
-            send_sem=f_ssem.at[u - NT, d],
-            recv_sem=f_rsem.at[u - NT, d],
+            dst_ref=r7.at[u - STEPPED, d],
+            send_sem=f_ssem.at[u - STEPPED, d],
+            recv_sem=f_rsem.at[u - STEPPED, d],
             device_id=(i ^ flip_of(d), j),
             device_id_type=MESH,
         )
@@ -297,7 +298,7 @@
         total = s[(u, core, *own)]
         for d in PIECES:
             direct(u, d).wait_recv()
-            total = total + r7[u - NT, d]
+            total = total + r7[u - STEPPED, d]
         s[(u, core, *own)] = total
 
     def finish_exchange(u, k):
@@ -330,11 +331,11 @@
             al[q0 * 8 : (q0 + 4) * 8, :] = lo
         prod = dot3(ah[...], al[...], eh[cols, :], el[cols, :])
         if t == 0:
-            gacc[...] = prod
+            gacc[h] = prod
         elif t < NT - 1:
-            gacc[...] += prod
+            gacc[h] += prod
         else:
-            total = (gacc[...] + prod).reshape(SLOTS, 8, 2 * M)
+            total = (gacc[h] + prod).reshape(SLOTS, 8, 2 * M)
             cross = total[:, :, M:]
             cross = jnp.concatenate([cross[:, 4:], cross[:, :4]], 1)
             g[h] = total[:, :, :M] + cross * sign
@@ -427,9 +428,9 @@
     def end_strips():
         for u in range(2 * NT):
             d2d(u).wait_send()
-            for d in PIECES if u >= NT else ():
+            for d in PIECES if u >= STEPPED else ():
                 direct(u, d).wait_send()
-            for k in range(3 if u < NT else 0):
+            for k in range(3 if u < STEPPED else 0):
                 for gi in range(3):
                     exchange(u, k, gi).wait_send()
 
@@ -493,11 +494,11 @@
     ("m", 3), ("d", 2), ("e", 0, 0),
     ("t",), ("d", 3),
     ("m", 4), ("e", 1, 0),
-    ("m", 5), ("d", 4), ("e", 0, 1), ("e", 2, 0), ("e", 3, 0),
-    ("m", 6), ("d", 5), ("e", 1, 1),
-    ("m", 7), ("d", 6), ("e", 2, 1), ("e", 3, 1), ("d", 7),
-    ("g",), ("e", 0, 2), ("c", 0), ("e", 1, 2), ("c", 1), ("e", 2, 2), ("c", 2), ("e", 3, 2), ("c", 3), ("s", 0),
-    ("f", 4), ("c", 4), ("f", 5), ("c", 5), ("f", 6), ("c", 6), ("w",), ("f", 7), ("c", 7), ("s", 1),
+    ("m", 5), ("e", 2, 0), ("e", 0, 1), ("d", 4),
+    ("m", 6), ("e", 1, 1), ("d", 5),
+    ("m", 7), ("e", 2, 1), ("d", 6), ("d", 7),
+    ("g",), ("e", 0, 2), ("c", 0), ("f", 4), ("c", 4), ("e", 1, 2), ("c", 1), ("e", 2, 2), ("c", 2), ("f", 3), ("c", 3), ("s", 0),
+    ("f", 5), ("c", 5), ("f", 6), ("c", 6), ("w",), ("f", 7), ("c", 7), ("s", 1),
     ("a", 0), ("x", 0), ("a", 1), ("x", 1), ("b", 0), ("y", 0), ("b", 1), ("y", 1),
 )
 
@@ -526,17 +527,17 @@
             pltpu.VMEM((2, F // 8, M), f32),
             pltpu.VMEM((u, 2, 2, 2, 2, 4, 8, CW), f32),
             pltpu.VMEM((u, 2, 2, 2, 4, 8, CW), f32),
-            pltpu.VMEM((NT, 2, 2, 4, 8, CW), f32),
-            pltpu.VMEM((NT, 2, 4, 8, CW), f32),
-            pltpu.VMEM((NT, 4, 8, CW), f32),
-            pltpu.VMEM((NT, 8, 4, 8, CW), f32),
+            pltpu.VMEM((STEPPED, 2, 2, 4, 8, CW), f32),
+            pltpu.VMEM((STEPPED, 2, 4, 8, CW), f32),
+            pltpu.VMEM((STEPPED, 4, 8, CW), f32),
+            pltpu.VMEM((u - STEPPED, 8, 4, 8, CW), f32),
             pltpu.VMEM((2, 4, 8, CW), f32),
             pltpu.VMEM((2, SLOTS, F), f32),
             pltpu.VMEM((F, 2 * M), bf16),
             pltpu.VMEM((F, 2 * M), bf16),
             pltpu.VMEM((SLOTS * 8, CW), bf16),
             pltpu.VMEM((SLOTS * 8, CW), bf16),
-            pltpu.VMEM((SLOTS * 8, 2 * M), f32),
+            pltpu.VMEM((2, SLOTS * 8, 2 * M), f32),
             pltpu.VMEM((2, SLOTS, 8, M), f32),
             pltpu.VMEM((2, 2, 8, 3, 8, M), f32),
             pltpu.VMEM((2, 8, 3, 8, M), f32),
@@ -546,10 +547,10 @@
             dma((6,)),
             dma((u,)),
             dma((u,)),
-            dma((NT, 3, 3)),
-            dma((NT, 3, 3)),
-            dma((NT, 8)),
-            dma((NT, 8)),
+            dma((STEPPED, 3, 3)),
+            dma((STEPPED, 3, 3)),
+            dma((u - STEPPED, 8)),
+            dma((u - STEPPED, 8)),
             dma((2, 16)),
             dma((2, 2, 8)),
             dma((2, 8)),

time: 53.9 us -> 54.6 us (1.013)
  Pallas kernels: 51.1 us -> 51.8 us
    pallas_call x1, Pallas kernels: 51.1 us -> 51.8 us  [per_device(): pl.pallas_call(kernel, out_shape=jax.ShapeDtypeStruct((3, 2, 8, M), f32),...]
where the time goes in v5:
time: 54.6 us; the launch traced here: 54.4 us
  Pallas kernels  51.8 us (95%)
  local copies, waits for them, and re-layouts  1.35 us (2%)
  between operations  1.31 us (2%)
    pallas_call x1, Pallas kernels, per_device(): pl.pallas_call(kernel, out_shape=jax.ShapeDtypeStruct((3, 2, 8, M), f32),...  51.8 us
    unnamed x1, local copies, waits for them, and re-layouts  1.35 us

profile of v5, /device:TPU:1, one launch (start us, length us, event | category | flops | bytes accessed | tf_op | source)
XLA Modules:
  0.0 54.4 jit_solution(15794597521624956703)
XLA Ops:
  1.3 51.8 %facet_to_subgrid.1 = f32[3,2,8,128]{3,2,1,0:T(8,128)} custom-call(f32[2,1024,1024]{2,1,0:T(8,128)} %x_hbm.1, s32[1]{0:T(128)S(6)} %copy.9.rest_0_, s32[1]{0:T(128)S(6)} %copy.10.rest_1_, s32[4]{0:T(128)} %rest_2_.1, s32[48]{0:T(128)} %rest_3_.1, s32[48]{0:T(128)} %rest_4_.1, s32[48]{0:T(128)} %rest_5_.1), custom_call_target="tpu_custom_call" | custom-call | tf_op jit(solution)/shard_map/facet_to_subgrid/pallas_call | solution.py:510
  53.1 1.3 %copy.11 = f32[3,2,8,128]{3,2,1,0:T(8,128)} copy(f32[3,2,8,128]{3,2,1,0:T(8,128)} %facet_to_subgrid.1) | data formatting | bytes 49152
